TPU v7x, 32 devices: a whole 2x2x4 slice. The times are simulated.
32 devices in a mesh: row: 16 (over z, x, core), blk: 2 (over y).
Axes of the slice: x: 2, y: 2, z: 4, core: 2. Of those that a mesh axis runs over, the one named last changes fastest.
Arguments:
- embeddings: bfloat16 [8192, 192], P(('row', 'blk')), may hold values from -30 to 30
- vectors: float32 [8192, 16], P(('row', 'blk')), may hold values from -6 to 6
Outputs:
- basis: float32 [8192, 16], P(('row', 'blk'))
- triangle: float32 [16, 16], replicated
All inputs are finite; a program needn't handle non-finite values.
Results may differ from a plain program's by a relative error of at most 0.0088.
Values may be sent and summed in bfloat16 or wider, within the bound.
A program may use at most 64 MiB of HBM per device.

v0:
```python
import jax
import jax.numpy as jnp
from jax import lax
from jax.sharding import PartitionSpec as P

sharpness = 10.0
epsilon = 1e-06


def normalize(embeddings):
    values = embeddings.astype(jnp.float32)
    return (values * lax.rsqrt(jnp.sum(values * values, axis=1, keepdims=True) + epsilon)).astype(
        jnp.bfloat16
    )


def affinity(block_rows, columns):
    scores = lax.dot_general(
        block_rows, columns, (((1,), (1,)), ((), ())), preferred_element_type=jnp.float32
    )
    return jnp.exp(sharpness * (scores - 1.0))


def gram_total(projected):
    local_gram = jnp.dot(projected.T, projected, precision=lax.Precision.HIGHEST)
    return lax.psum(local_gram, ("row", "blk"))


def finish(projected, gram_matrix):
    factor = jnp.linalg.cholesky(gram_matrix)
    basis = jax.scipy.linalg.solve_triangular(factor, projected.T, lower=True).T
    return (basis, factor.T)


def per_device(embeddings, vectors):
    unit_rows = normalize(embeddings)
    local_rows = unit_rows.shape[0]
    columns_out = vectors.shape[1]
    everything = lax.all_gather(unit_rows, ("row", "blk"), axis=0, tiled=True)
    column_blocks = everything.reshape(16, -1, everything.shape[1])

    def add_degree(running, columns):
        return (running + jnp.sum(affinity(unit_rows, columns), axis=1), None)

    degree, unused = lax.scan(add_degree, jnp.zeros((local_rows,), jnp.float32), column_blocks)
    inverse_root = lax.rsqrt(degree)
    weighted = (vectors * inverse_root[:, None]).astype(jnp.bfloat16)
    all_weighted = lax.all_gather(weighted, ("row", "blk"), axis=0, tiled=True)
    weight_blocks = all_weighted.reshape(16, -1, columns_out)

    def add_image(running, column_pair):
        tile = affinity(unit_rows, column_pair[0]).astype(jnp.bfloat16)
        return (running + jnp.dot(tile, column_pair[1], preferred_element_type=jnp.float32), None)

    summed, unused = lax.scan(
        add_image, jnp.zeros((local_rows, columns_out), jnp.float32), (column_blocks, weight_blocks)
    )
    projected = summed * inverse_root[:, None]
    gram_matrix = gram_total(projected)
    return finish(projected, gram_matrix)


def solution(mesh):
    placed = (P(("row", "blk"), None), P(("row", "blk"), None))
    return jax.shard_map(
        per_device,
        mesh=mesh,
        in_specs=placed,
        out_specs=(P(("row", "blk"), None), P()),
        check_vma=False,
    )
```

profile of v0, /device:TPU:10, one launch (start us, length us, event | category | flops | bytes accessed | tf_op | source)
XLA Modules:
  0.0 237.3 jit_solution(9475091258592382301)
XLA Ops:
  7.2 0.0 copy-start
  7.2 0.0 all-gather.2.cloned.1.call-start
  7.2 1.0 copy.4
  8.2 0.1 fusion.23
  8.3 0.8 fusion.24
  9.1 0.0 all-gather.2.cloned.1.call-update
  9.1 64.3 %all-gather.2.cloned.1.call-done = bf16[8192,192]{1,0:T(8,128)(2,1)} async-done(((bf16[256,192]{1,0:T(8,128)(2,1)}), bf16[8192,192]{1,0:T(8,128)(2,1)}) %all-gather.2.cloned.1.call-update) | async-done | bytes 3145744 | tf_op jit(solution)/shard_map/all_gather | solution.py:39
  73.5 21.6 %while.26 = (s32[]{:T(128)}, f32[256]{0:T(256)S(1)}, bf16[16,512,192]{2,1,0:T(8,128)(2,1)}, bf16[256,192]{1,0:T(8,128)(2,1)}, s32[]{:T(128)}, /*index=5*/s32[]{:T(128)}) while((s32[]{:T(128)}, f32[256]{0:T(256)S(1)}, bf16[16,512,192]{2,1,0:T(8,128)(2,1)}, bf16[256,192]{1,0:T(8,128)(2,1)}, s32[]{:T(128)}, /*index=5*/s32[]{:T(128)}) %tuple.72), condition=%wide.region_3.4_spmd.clone, body=%wide.region_1.3_spmd.clone.sunk | while | flops 50725120 | bytes 397903 | solution.py:45
  73.5 1.3 fusion.45
  74.8 1.3 fusion.45
  76.2 1.3 fusion.45
  77.5 1.3 fusion.45
  78.9 1.3 fusion.45
  80.2 1.3 fusion.45
  81.6 1.3 fusion.45
  82.9 1.3 fusion.45
  84.3 1.3 fusion.45
  85.6 1.3 fusion.45
  87.0 1.3 fusion.45
  88.3 1.3 fusion.45
  89.7 1.3 fusion.45
  91.0 1.3 fusion.45
  92.4 1.3 fusion.45
  93.7 1.3 fusion.45
  95.1 0.0 copy-done
  95.1 48.5 %all_gather.7 = bf16[8192,16]{0,1:T(8,128)(2,1)S(1)} all-gather(bf16[256,16]{0,1:T(8,128)(2,1)S(1)} %multiply_convert_fusion), channel_id=1, replica_groups=mesh['row'=16,'blk'=2] {'row','blk'}, dimensions={0}, use_global_device_ids=true | all-gather | bytes 270336 | tf_op jit(solution)/shard_map/all_gather | solution.py:48
  143.6 22.8 %while.27 = (s32[]{:T(128)}, f32[256,16]{0,1:T(8,128)S(1)}, bf16[16,512,192]{2,1,0:T(8,128)(2,1)}, bf16[256,192]{1,0:T(8,128)(2,1)}, bf16[16,512,16]{1,2,0:T(8,128)(2,1)S(1)}, /*index=5*/s32[]{:T(128)}, s32[]{:T(128)}) while((s32[]{:T(128)}, f32[256,16]{0,1:T(8,128)S(1)}, bf16[16,512,192]{2,1,0:T(8,128)(2,1)}, ...), condition=%wide.region_5.6_spmd.clone, body=%wide.region_4.5_spmd.clone.sunk | while | flops 54927360 | bytes 443479 | solution.py:55
  143.6 1.4 fusion.49
  145.0 1.4 fusion.49
  146.4 1.4 fusion.49
  147.9 1.4 fusion.49
  149.3 1.4 fusion.49
  150.7 1.4 fusion.49
  152.1 1.4 fusion.49
  153.6 1.4 fusion.49
  155.0 1.4 fusion.49
  156.4 1.4 fusion.49
  157.8 1.4 fusion.49
  159.3 1.4 fusion.49
  160.7 1.4 fusion.49
  162.1 1.4 fusion.49
  163.5 1.4 fusion.49
  165.0 1.4 fusion.49
  166.4 0.1 fusion.27
  166.5 58.4 %psum.7 = f32[16,16]{0,1:T(8,128)S(1)} all-reduce(f32[16,16]{0,1:T(8,128)S(1)} %fusion.27), channel_id=1, replica_groups=mesh['row'=16,'blk'=2] {'row','blk'}, use_global_device_ids=true, to_apply=%region_6.7 | all-reduce | flops 256 | bytes 2048 | tf_op jit(solution)/shard_map/psum | solution.py:26
  224.9 0.1 copy.7
  225.0 1.5 cholesky.16
  226.4 0.6 compare_reduce_fusion
  227.1 0.6 fusion.33
  227.7 1.2 custom-call.7
  229.0 0.8 fusion.25
  229.8 0.7 copy.8
  (24 shorter events, 0.3 us)
Async XLA Ops:
  7.2 87.9 %copy-start = (f32[256,16]{0,1:T(8,128)S(1)}, f32[256,16]{0,1:T(8,128)}, u32[]{:S(2)}) copy-start(f32[256,16]{0,1:T(8,128)} %param.7) | copy-start | bytes 49156
  7.2 66.3 %all-gather.2.cloned.1.call-start = ((), (), s32[]{:S(2)}) async-start(), calls=%async_computation | async-start | bytes 4325376 | tf_op jit(solution)/shard_map/all_gather | solution.py:39
Sparse Core Ops, SparseCore 0:
  10.9 62.5 all-gather.1
where the time goes:
time: 238 us; the launch traced here: 237 us
  blocking collectives  107 us (45%)
  waiting for transfers between devices  64.4 us (27%)
  matrix products  44.8 us (19%)
  between operations  14.1 us (6%)
  other arithmetic  5.09 us (2%)
    all_gather x1, waiting for transfers between devices, per_device(): everything = lax.all_gather(unit_rows, ('row', 'blk'), axis=0, tiled=True)  64.3 us
    psum x1, blocking collectives, gram_total(): return lax.psum(local_gram, ('row', 'blk'))  58.4 us
    all_gather x1, blocking collectives, per_device(): all_weighted = lax.all_gather(weighted, ('row', 'blk'), axis=0, tiled=True)  48.5 us
    dot_general x16, matrix products, add_image(): jnp.dot(tile, column_pair[1], preferred_element_type=jnp.float32)  22.8 us
    dot_general x16, matrix products, affinity(): lax.dot_general(block_rows, columns, (((1,), (1,)), ((), ())), preferred_...  21.1 us
  transfers between devices with their start and end apart: 1, of which 1 were waited for; matrix products, arithmetic and copies ran while one was open for 0% of the time, Pallas kernels for 0%

commit v1 on v0

--- a/solution.py
+++ b/solution.py
@@ -36,7 +36,14 @@
     unit_rows = normalize(embeddings)
     local_rows = unit_rows.shape[0]
     columns_out = vectors.shape[1]
-    everything = lax.all_gather(unit_rows, ("row", "blk"), axis=0, tiled=True)
+    ways, here = (lax.axis_size(("row", "blk")), lax.axis_index(("row", "blk")))
+    everything, reach = (unit_rows, 1)
+    while reach < ways:
+        theirs = lax.ppermute(everything, ("row", "blk"), [(d, d ^ reach) for d in range(ways)])
+        mine_first = jnp.concatenate([everything, theirs], axis=0)
+        theirs_first = jnp.concatenate([theirs, everything], axis=0)
+        everything = jnp.where(here & reach == 0, mine_first, theirs_first)
+        reach = 2 * reach
     column_blocks = everything.reshape(16, -1, everything.shape[1])
 
     def add_degree(running, columns):

time: 238 us -> 276 us (1.16)
  waiting for transfers between devices: 64.4 us -> 99.1 us
  between operations: 14.1 us -> 0.78 us
  other arithmetic: 5.09 us -> 10.7 us
  starting transfers between devices: 0.04 us -> 5.42 us
  local copies, waits for them, and re-layouts: 1.75 us -> 4.75 us
  blocking collectives: 107 us -> 110 us
    ppermute x0 -> x5, waiting for transfers between devices: none -> 99.1 us  [per_device(): lax.ppermute(everything, ('row', 'blk'), [(d, d ^ reach) for d in range(w...]
    all_gather x1 -> x0, waiting for transfers between devices: 64.3 us -> none  [per_device(): everything = lax.all_gather(unit_rows, ('row', 'blk'), axis=0, tiled=True)]
    ppermute x0 -> x5, starting transfers between devices: none -> 5.42 us  [per_device(): lax.ppermute(everything, ('row', 'blk'), [(d, d ^ reach) for d in range(w...]
    select_n x0 -> x5, other arithmetic: none -> 4.66 us  [per_device(): everything = jnp.where(here & reach == 0, mine_first, theirs_first)]
    unnamed x4 -> x7, local copies, waits for them, and re-layouts: 1.66 us -> 4.66 us
  transfers between devices with their start and end apart: 1 -> 5, of which waited for: 1 -> 5; matrix products, arithmetic and copies ran while one was open for 0% -> 0% of each run, Pallas kernels for 0% -> 0%
where the time goes in v1:
time: 276 us; the launch traced here: 274 us
  blocking collectives  110 us (40%)
  waiting for transfers between devices  99.1 us (36%)
  matrix products  43.7 us (16%)
  other arithmetic  10.7 us (4%)
  starting transfers between devices  5.42 us (2%)
  local copies, waits for them, and re-layouts  4.75 us (2%)
    ppermute x5, waiting for transfers between devices, per_device(): lax.ppermute(everything, ('row', 'blk'), [(d, d ^ reach) for d in range(w...  99.1 us
    psum x1, blocking collectives, gram_total(): return lax.psum(local_gram, ('row', 'blk'))  59.6 us
    all_gather x1, blocking collectives, per_device(): all_weighted = lax.all_gather(weighted, ('row', 'blk'), axis=0, tiled=True)  50 us
    dot_general x16, matrix products, add_image(): jnp.dot(tile, column_pair[1], preferred_element_type=jnp.float32)  22.2 us
    dot_general x16, matrix products, affinity(): lax.dot_general(block_rows, columns, (((1,), (1,)), ((), ())), preferred_...  20.5 us
  transfers between devices with their start and end apart: 5, of which 5 were waited for; matrix products, arithmetic and copies ran while one was open for 0% of the time, Pallas kernels for 0%

profile of v1, /device:TPU:10, one launch (start us, length us, event | category | flops | bytes accessed | tf_op | source)
XLA Modules:
  0.0 274.5 jit_solution(15880969397334541634)
XLA Ops:
  0.6 0.9 fusion.23
  1.6 0.9 fusion.24
  2.5 1.6 collective-permute-start
  4.1 3.1 %collective-permute-done = bf16[256,192]{0,1:T(8,128)(2,1)S(1)} collective-permute-done((bf16[256,192]{0,1:T(8,128)(2,1)S(1)}, bf16[256,192]{0,1:T(8,128)(2,1)S(1)}, u32[]{:S(2)}, u32[]{:S(2)}) %collective-permute-start) | collective-permute-done | bytes 98336 | tf_op jit(solution)/shard_map/ppermute | solution.py:42
  7.2 0.1 maximum_select_fusion.4
  7.3 0.1 collective-permute-start.1
  7.3 1.4 collective-permute-done.1
  8.8 0.1 maximum_select_fusion.3
  8.9 0.6 collective-permute-start.2
  9.5 10.6 %collective-permute-done.2 = bf16[1024,192]{0,1:T(8,128)(2,1)S(1)} collective-permute-done((bf16[1024,192]{0,1:T(8,128)(2,1)S(1)}, bf16[1024,192]{0,1:T(8,128)(2,1)S(1)}, u32[]{:S(2)}, u32[]{:S(2)}) %collective-permute-start.2) | collective-permute-done | bytes 393248 | tf_op jit(solution)/shard_map/ppermute | solution.py:42
  20.1 0.3 maximum_select_fusion.2
  20.4 0.5 collective-permute-start.3
  20.9 18.3 %collective-permute-done.3 = bf16[2048,192]{0,1:T(8,128)(2,1)S(1)} collective-permute-done((bf16[2048,192]{0,1:T(8,128)(2,1)S(1)}, bf16[2048,192]{0,1:T(8,128)(2,1)S(1)}, u32[]{:S(2)}, u32[]{:S(2)}) %collective-permute-start.3) | collective-permute-done | bytes 786464 | tf_op jit(solution)/shard_map/ppermute | solution.py:42
  39.2 0.5 maximum_select_fusion.1
  39.7 2.7 collective-permute-start.4
  42.4 0.1 copy.12
  42.5 65.7 %collective-permute-done.4 = bf16[4096,192]{0,1:T(8,128)(2,1)} collective-permute-done((bf16[4096,192]{0,1:T(8,128)(2,1)S(1)}, bf16[4096,192]{0,1:T(8,128)(2,1)}, u32[]{:S(2)}, u32[]{:S(2)}) %collective-permute-start.4) | collective-permute-done | bytes 1572896 | tf_op jit(solution)/shard_map/ppermute | solution.py:42
  108.2 3.7 %maximum_select_fusion = bf16[8192,192]{0,1:T(8,128)(2,1)S(1)} fusion(bf16[4096,192]{0,1:T(8,128)(2,1)} %collective-permute-done.4, bf16[4096,192]{0,1:T(8,128)(2,1)} %copy-done, pred[]{:T(512)S(6)} %eq.15), kind=kLoop, calls=%fused_computation.23 | loop fusion | flops 14155776 | bytes 6291457 | tf_op jit(solution)/shard_map/jit(_where)/select_n | solution.py:45
  111.9 3.9 %copy.18 = bf16[8192,192]{1,0:T(8,128)(2,1)} copy(bf16[8192,192]{0,1:T(8,128)(2,1)S(1)} %maximum_select_fusion) | data formatting | bytes 6291456
  115.8 21.0 %while.26 = (s32[]{:T(128)}, f32[256]{0:T(256)S(1)}, bf16[16,512,192]{2,1,0:T(8,128)(2,1)}, bf16[256,192]{1,0:T(8,128)(2,1)S(1)}, s32[]{:T(128)}, /*index=5*/s32[]{:T(128)}) while((s32[]{:T(128)}, f32[256]{0:T(256)S(1)}, bf16[16,512,192]{2,1,0:T(8,128)(2,1)}, bf16[256,192]{1,0:T(8,128)(2,1)S(1)}, s32[]{:T(128)}, ...), condition=%wide.region_3.4_spmd.clone, body=%wide.region_1.3_spmd.clone.sunk | while | flops 50725120 | bytes 365135 | solution.py:52
  115.8 1.3 fusion.45
  117.1 1.3 fusion.45
  118.4 1.3 fusion.45
  119.7 1.3 fusion.45
  121.1 1.3 fusion.45
  122.4 1.3 fusion.45
  123.7 1.3 fusion.45
  125.0 1.3 fusion.45
  126.3 1.3 fusion.45
  127.6 1.3 fusion.45
  129.0 1.3 fusion.45
  130.3 1.3 fusion.45
  131.6 1.3 fusion.45
  132.9 1.3 fusion.45
  134.2 1.3 fusion.45
  135.5 1.3 fusion.45
  136.9 0.0 copy-done.1
  136.9 50.0 %all_gather.3 = bf16[8192,16]{0,1:T(8,128)(2,1)S(1)} all-gather(bf16[256,16]{0,1:T(8,128)(2,1)S(1)} %multiply_convert_fusion), channel_id=1, replica_groups=mesh['row'=16,'blk'=2] {'row','blk'}, dimensions={0}, use_global_device_ids=true | all-gather | bytes 270336 | tf_op jit(solution)/shard_map/all_gather | solution.py:55
  186.9 22.2 %while.27 = (s32[]{:T(128)}, f32[256,16]{0,1:T(8,128)S(1)}, bf16[16,512,192]{2,1,0:T(8,128)(2,1)}, bf16[256,192]{1,0:T(8,128)(2,1)S(1)}, bf16[16,512,16]{1,2,0:T(8,128)(2,1)S(1)}, /*index=5*/s32[]{:T(128)}, s32[]{:T(128)}) while((s32[]{:T(128)}, f32[256,16]{0,1:T(8,128)S(1)}, bf16[16,512,192]{2,1,0:T(8,128)(2,1)}, ...), condition=%wide.region_5.6_spmd.clone, body=%wide.region_4.5_spmd.clone.sunk | while | flops 54927360 | bytes 443479 | solution.py:62
  186.9 1.4 fusion.49
  188.3 1.4 fusion.49
  189.7 1.4 fusion.49
  191.1 1.4 fusion.49
  192.4 1.4 fusion.49
  193.8 1.4 fusion.49
  195.2 1.4 fusion.49
  196.6 1.4 fusion.49
  198.0 1.4 fusion.49
  199.4 1.4 fusion.49
  200.8 1.4 fusion.49
  202.2 1.4 fusion.49
  203.6 1.4 fusion.49
  205.0 1.4 fusion.49
  206.3 1.4 fusion.49
  207.7 1.4 fusion.49
  209.1 0.1 fusion.27
  209.3 59.6 %psum.7 = f32[16,16]{0,1:T(8,128)S(1)} all-reduce(f32[16,16]{0,1:T(8,128)S(1)} %fusion.27), channel_id=1, replica_groups=mesh['row'=16,'blk'=2] {'row','blk'}, use_global_device_ids=true, to_apply=%region_6.7 | all-reduce | flops 256 | bytes 2048 | tf_op jit(solution)/shard_map/psum | solution.py:26
  268.9 0.1 copy.15
  269.0 1.5 cholesky.16
  270.5 0.6 compare_reduce_fusion
  271.1 0.6 fusion.33
  271.8 1.2 custom-call.7
  273.0 0.8 fusion.25
  273.8 0.7 copy.16
  (27 shorter events, 0.3 us)
Async XLA Ops:
  2.5 4.7 %collective-permute-start = (bf16[256,192]{0,1:T(8,128)(2,1)S(1)}, bf16[256,192]{0,1:T(8,128)(2,1)S(1)}, u32[]{:S(2)}, u32[]{:S(2)}) collective-permute-start(bf16[256,192]{0,1:T(8,128)(2,1)S(1)} %fusion.24), channel_id=1, source_target_pairs={{0,1},{1,0},{2,3},{3,2},{4,5},{5,4},{6,7},{7,6},{8,9},{9,8},{10,11... | collective-permute-start | bytes 294920 | tf_op jit(solution)/shard_map/ppermute | solution.py:42
  7.3 1.5 collective-permute-start.1
  8.9 11.2 %collective-permute-start.2 = (bf16[1024,192]{0,1:T(8,128)(2,1)S(1)}, bf16[1024,192]{0,1:T(8,128)(2,1)S(1)}, u32[]{:S(2)}, u32[]{:S(2)}) collective-permute-start(bf16[1024,192]{0,1:T(8,128)(2,1)S(1)} %maximum_select_fusion.3), channel_id=1, source_target_pairs={{0,4},{1,5},{2,6},{3,7},{4,0},{5,1},{6,2},{7,3},{8,12},{9,13},{10,... | collective-permute-start | bytes 1179656 | tf_op jit(solution)/shard_map/ppermute | solution.py:42
  20.4 18.8 %collective-permute-start.3 = (bf16[2048,192]{0,1:T(8,128)(2,1)S(1)}, bf16[2048,192]{0,1:T(8,128)(2,1)S(1)}, u32[]{:S(2)}, u32[]{:S(2)}) collective-permute-start(bf16[2048,192]{0,1:T(8,128)(2,1)S(1)} %maximum_select_fusion.2), channel_id=1, source_target_pairs={{0,8},{1,9},{2,10},{3,11},{4,12},{5,13},{6,14},{7,15},{8,0},{9,1},... | collective-permute-start | bytes 2359304 | tf_op jit(solution)/shard_map/ppermute | solution.py:42
  39.7 2.8 %copy-start = (bf16[4096,192]{0,1:T(8,128)(2,1)}, bf16[4096,192]{0,1:T(8,128)(2,1)S(1)}, u32[]{:S(2)}) copy-start(bf16[4096,192]{0,1:T(8,128)(2,1)S(1)} %maximum_select_fusion.1) | copy-start | bytes 4718596
  39.7 68.5 %collective-permute-start.4 = (bf16[4096,192]{0,1:T(8,128)(2,1)S(1)}, bf16[4096,192]{0,1:T(8,128)(2,1)}, u32[]{:S(2)}, u32[]{:S(2)}) collective-permute-start(bf16[4096,192]{0,1:T(8,128)(2,1)S(1)} %maximum_select_fusion.1), channel_id=1, source_target_pairs={{0,16},{1,17},{2,18},{3,19},{4,20},{5,21},{6,22},{7,23},{8,24},{9,... | collective-permute-start | bytes 4718600 | tf_op jit(solution)/shard_map/ppermute | solution.py:42
  115.8 21.1 %copy-start.1 = (f32[256,16]{0,1:T(8,128)S(1)}, f32[256,16]{0,1:T(8,128)}, u32[]{:S(2)}) copy-start(f32[256,16]{0,1:T(8,128)} %param.7) | copy-start | bytes 49156
